TPU v7x, 32 devices: a whole 2x2x4 slice. The times are simulated.
32 devices in a mesh: section: 2 (over y), ep: 16 (over z, x, core).
Axes of the slice: x: 2, y: 2, z: 4, core: 2. Of those that a mesh axis runs over, the one named last changes fastest.
Arguments:
- inputs: bfloat16 [2, 2048, 1536], P('section', 'ep'), may hold values from -6 to 6
- upstream: bfloat16 [2, 2048, 1536], P('section', 'ep'), may hold values from -6 to 6
- gate_saved: bfloat16 [2, 2048, 8, 384], P('section', 'ep'), may hold values from -6 to 6
- expert_ids: int32 [2, 2048, 8], P('section', 'ep'), may hold values from 0 to 31, all different within a row; in each aligned block of 128 rows (0 to 127, 128 to 255, ..., all dimensions but the last counted through in order) at most 48 rows name the same one
- route_weights: float32 [2, 2048, 8], P('section', 'ep'), may hold values from 0.05 to 0.5
- w_up: bfloat16 [2, 32, 1536, 384], P('section', 'ep'), may hold values from -0.15625 to 0.15625
- w_down: bfloat16 [2, 32, 384, 1536], P('section', 'ep'), may hold values from -0.3125 to 0.3125
Outputs:
- delivered: bfloat16 [2, 2048, 1536], P('section', 'ep')
- grad_up: bfloat16 [2, 32, 1536, 384], P('section', 'ep')
- grad_down: bfloat16 [2, 32, 384, 1536], P('section', 'ep')
Inputs may be any that keep to these rules, and one draw needn't show every extreme that they name: `expert_ids`: each row names 8 different experts. In the rows of one device no expert is named more than 48 times, and in every draw some expert is named exactly 48 times in the rows of some device; every expert is named somewhere.
All inputs are finite; a program needn't handle non-finite values.
Results may differ from a plain program's by a relative error of at most 0.012.
Values may be sent and summed in bfloat16 or wider, within the bound.
A program may use at most 192 MiB of HBM per device.

v0:
```python
import jax
import jax.numpy as jnp
from jax import lax
from jax.sharding import PartitionSpec as P


def from_behind(block, axis, distance):
    devices = range(lax.axis_size(axis))
    route = [((i - distance) % len(devices), i) for i in devices]
    return lax.ppermute(block, axis, route)


def expert_grads(x_rows, gate_rows, cot_rows, up_weight, down_weight):
    activation = jax.nn.silu(gate_rows.astype(jnp.float32))
    up_value = jnp.dot(x_rows, up_weight, preferred_element_type=jnp.float32)
    hidden = (activation * up_value).astype(jnp.bfloat16)
    grad_down = lax.dot_general(
        hidden, cot_rows, (((0,), (0,)), ((), ())), preferred_element_type=jnp.float32
    )
    grad_hidden = lax.dot_general(
        cot_rows, down_weight, (((1,), (1,)), ((), ())), preferred_element_type=jnp.float32
    )
    grad_rows = (grad_hidden * activation).astype(jnp.bfloat16)
    grad_up = lax.dot_general(
        x_rows, grad_rows, (((0,), (0,)), ((), ())), preferred_element_type=jnp.float32
    )
    slot_grad = lax.dot_general(
        grad_rows, up_weight, (((1,), (1,)), ((), ())), preferred_element_type=jnp.float32
    )
    return (grad_up, grad_down, slot_grad.astype(jnp.bfloat16))


def body(inputs, upstream, gate_saved, expert_ids, route_weights, w_up, w_down):
    tokens_here = inputs[0]
    ep_size = lax.axis_size("ep")
    local_count = w_up.shape[1]
    experts = local_count * ep_size
    tok_count = expert_ids.shape[1]
    top_count = expert_ids.shape[2]
    capacity = 3 * tok_count * top_count // (2 * experts)
    feature_width = inputs.shape[2]
    hidden_width = w_up.shape[3]
    slot_total = tok_count * top_count
    flat_ids = expert_ids[0].reshape(slot_total)
    onehot = (flat_ids[:, None] == jnp.arange(experts, dtype=jnp.int32)[None, :]).astype(jnp.int32)
    position = jnp.sum(jnp.cumsum(onehot, axis=0) * onehot, axis=1) - 1
    slot_index = flat_ids * capacity + position
    sources = jnp.full((experts * capacity,), slot_total, jnp.int32)
    sources = sources.at[slot_index].set(jnp.arange(slot_total, dtype=jnp.int32))
    token_of = sources // top_count
    x_send = jnp.take(tokens_here, token_of, axis=0, mode="fill", fill_value=0)
    x_send = x_send.reshape(ep_size, local_count, capacity, feature_width)
    gate_send = jnp.take(
        gate_saved[0].reshape(slot_total, hidden_width), sources, axis=0, mode="fill", fill_value=0
    )
    gate_send = gate_send.reshape(ep_size, local_count, capacity, hidden_width)
    route_scale = jnp.take(
        route_weights[0].reshape(slot_total), sources, axis=0, mode="fill", fill_value=0
    )
    cotangent = from_behind(upstream, "section", -1)[0]
    cot_rows = jnp.take(cotangent, token_of, axis=0, mode="fill", fill_value=0)
    cot_send = (route_scale[:, None] * cot_rows.astype(jnp.float32)).astype(jnp.bfloat16)
    cot_send = cot_send.reshape(ep_size, local_count, capacity, feature_width)
    x_recv, gate_recv, cot_recv = (
        lax.all_to_all(x_send, "ep", split_axis=0, concat_axis=2, tiled=True),
        lax.all_to_all(gate_send, "ep", split_axis=0, concat_axis=2, tiled=True),
        lax.all_to_all(cot_send, "ep", split_axis=0, concat_axis=2, tiled=True),
    )
    up_grads = []
    down_grads = []
    slot_grads = []
    for expert_number in range(local_count):
        x_rows = x_recv[0, expert_number]
        gate_rows = gate_recv[0, expert_number]
        expert_cot = cot_recv[0, expert_number]
        up_weight = w_up[0, expert_number]
        down_weight = w_down[0, expert_number]
        grad_up, grad_down, slot_grad = expert_grads(
            x_rows, gate_rows, expert_cot, up_weight, down_weight
        )
        up_grads.append(grad_up.astype(jnp.bfloat16))
        down_grads.append(grad_down.astype(jnp.bfloat16))
        slot_grads.append(slot_grad)
    slot_block = jnp.stack(slot_grads, axis=0)[None]
    returned = lax.all_to_all(slot_block, "ep", split_axis=2, concat_axis=0, tiled=True)
    returned = returned.reshape(experts * capacity, feature_width)
    token_slots = jnp.take(returned, slot_index, axis=0).reshape(
        tok_count, top_count, feature_width
    )
    layer_grad = jnp.sum(token_slots.astype(jnp.float32), axis=1).astype(jnp.bfloat16)
    delivered = from_behind(layer_grad[None], "section", -1)
    grad_up_all = jnp.stack(up_grads, axis=0)[None]
    grad_down_all = jnp.stack(down_grads, axis=0)[None]
    return (delivered, grad_up_all, grad_down_all)


def solution(mesh):
    return jax.shard_map(
        body,
        mesh=mesh,
        in_specs=(
            P("section", "ep", None),
            P("section", "ep", None),
            P("section", "ep", None, None),
            P("section", "ep", None),
            P("section", "ep", None),
            P("section", "ep", None, None),
            P("section", "ep", None, None),
        ),
        out_specs=(
            P("section", "ep", None),
            P("section", "ep", None, None),
            P("section", "ep", None, None),
        ),
        check_vma=False,
    )
```

profile of v0, /device:TPU:10, one launch (start us, length us, event | category | flops | bytes accessed | tf_op | source)
XLA Modules:
  0.0 420.3 jit_solution(3634731702890086735)
XLA Ops:
  0.6 0.9 copy.35
  1.7 0.7 broadcast_multiply_fusion
  2.4 9.0 %reduce-window.6 = s32[32,8,128]{2,1,0:T(8,128)S(1)} reduce-window(s32[32,8,128]{2,1,0:T(8,128)S(1)} %fusion.43, s32[]{:T(128)} %constant.74.clone.1), window={size=1x1x128 pad=0_0x0_0x127_0}, to_apply=%region_0.0 | reduce-window | flops 4161536 | bytes 262148 | tf_op jit(solution)/shard_map/reduce-window
  11.5 0.1 copy.37
  12.1 4.3 %scatter_custom_fusion = s32[1536]{0:T(1024)S(1)} fusion(s32[1024]{0:T(1024)S(1)} %bitcast.173, s32[1024]{0:T(1024)S(1)} %iota.11, s32[]{:T(128)} %constant.78.clone.1), kind=kCustom, calls=%fused_computation.90 | custom fusion | bytes 6148 | tf_op jit(solution)/shard_map/scatter | solution.py:49
  16.5 0.8 copy.42
  17.4 5.9 %gather_fusion = f32[1536]{0:T(1024)S(1)} fusion(f32[1024]{0:T(1024)S(1)} %reshape_squeeze.10, s32[2048]{0:T(1024)S(1)} %pad_clamp_fusion.1), kind=kCustom, calls=%fused_computation.2 | custom fusion | bytes 18432 | tf_op jit(solution)/shard_map/jit(_take)/gather | solution.py:57
  23.4 4.7 %gather_fusion.1 = bf16[1536,384]{1,0:T(8,128)(2,1)S(1)} fusion(bf16[1024,384]{1,0:T(8,128)(2,1)S(1)} %bitcast.149, s32[2048]{0:T(1024)S(1)} %pad_clamp_fusion.1), kind=kCustom, calls=%fused_computation.3 | custom fusion | bytes 2365440 | tf_op jit(solution)/shard_map/jit(_take)/gather | solution.py:53
  28.1 1.3 broadcast_select_fusion.1
  29.4 6.2 %all-to-all-start.1 = ((bf16[16,2,48,384]{3,2,1,0:T(8,128)(2,1)}), bf16[16,2,48,384]{3,2,1,0:T(8,128)(2,1)S(1)}, u32[]{:S(2)}, u32[]{:S(2)}) async-start(bf16[16,2,48,384]{3,2,1,0:T(8,128)(2,1)} %broadcast_select_fusion.1), calls=%async_computation.1 | async-start | bytes 2359296 | tf_op jit(solution)/shard_map/all_to_all | solution.py:66
  35.6 1.6 collective-permute-start
  37.2 9.6 %collective-permute-done = bf16[1,128,1536]{2,1,0:T(8,128)(2,1)S(1)} collective-permute-done((bf16[1,128,1536]{2,1,0:T(8,128)(2,1)S(1)}, bf16[1,128,1536]{2,1,0:T(8,128)(2,1)S(1)}, u32[]{:S(2)}, u32[]{:S(2)}) %collective-permute-start) | collective-permute-done | bytes 393248 | tf_op jit(solution)/shard_map/ppermute | solution.py:10
  46.8 6.3 %gather_fusion.3 = bf16[1536,1536]{1,0:T(8,128)(2,1)} fusion(bf16[128,1536]{1,0:T(8,128)(2,1)S(1)} %bitcast.151, s32[2048]{0:T(1024)S(1)} %pad_clamp_fusion), kind=kCustom, calls=%fused_computation.clone | custom fusion | bytes 9443328 | tf_op jit(solution)/shard_map/jit(_take)/gather | solution.py:61
  53.2 4.6 %multiply_convert_fusion = bf16[1536,1536]{1,0:T(8,128)(2,1)} fusion(bf16[1536,1536]{1,0:T(8,128)(2,1)} %gather_fusion.3, f32[1536]{0:T(1024)S(1)} %get-tuple-element.6, pred[1536]{0:T(1024)(128)(4,1)S(1)} %get-tuple-element.4), kind=kLoop, calls=%fused_computation.6 | loop fusion | flops 9437184 | bytes 9444864 | tf_op jit(solution)/shard_map/convert_element_type | solution.py:62
  57.7 5.4 %all-to-all-done.1 = bf16[16,2,48,384]{3,2,1,0:T(8,128)(2,1)S(1)} async-done(((bf16[16,2,48,384]{3,2,1,0:T(8,128)(2,1)}), bf16[16,2,48,384]{3,2,1,0:T(8,128)(2,1)S(1)}, u32[]{:S(2)}, u32[]{:S(2)}) %all-to-all-start.1) | async-done | bytes 1179680 | tf_op jit(solution)/shard_map/all_to_all | solution.py:66
  63.1 5.1 %all-to-all-start = ((bf16[16,2,48,1536]{3,2,1,0:T(8,128)(2,1)}), bf16[16,2,48,1536]{3,2,1,0:T(8,128)(2,1)}, u32[]{:S(2)}, u32[]{:S(2)}) async-start(bf16[16,2,48,1536]{3,2,1,0:T(8,128)(2,1)} %bitcast.154), calls=%async_computation | async-start | bytes 9437184 | tf_op jit(solution)/shard_map/all_to_all | solution.py:67
  68.3 6.2 %gather_fusion.4 = bf16[1536,1536]{1,0:T(8,128)(2,1)} fusion(bf16[128,1536]{1,0:T(8,128)(2,1)S(1)} %bitcast.150, s32[2048]{0:T(1024)S(1)} %pad_clamp_fusion), kind=kCustom, calls=%fused_computation.1.clone | custom fusion | bytes 9443328 | tf_op jit(solution)/shard_map/jit(_take)/gather | solution.py:51
  74.5 4.9 %broadcast_select_fusion = bf16[1536,1536]{1,0:T(8,128)(2,1)} fusion(bf16[1536,1536]{1,0:T(8,128)(2,1)} %gather_fusion.4, pred[1536]{0:T(1024)(128)(4,1)S(1)} %get-tuple-element.4), kind=kLoop, calls=%fused_computation.8 | loop fusion | flops 2359296 | bytes 9438720 | tf_op jit(solution)/shard_map/jit(_take)/select_n | solution.py:51
  79.4 92.2 %all-to-all-done = bf16[16,2,48,1536]{3,2,1,0:T(8,128)(2,1)} async-done(((bf16[16,2,48,1536]{3,2,1,0:T(8,128)(2,1)}), bf16[16,2,48,1536]{3,2,1,0:T(8,128)(2,1)}, u32[]{:S(2)}, u32[]{:S(2)}) %all-to-all-start) | async-done | bytes 4718624 | tf_op jit(solution)/shard_map/all_to_all | solution.py:67
  171.7 5.1 %all-to-all-start.3 = ((bf16[16,2,48,1536]{3,2,1,0:T(8,128)(2,1)}), bf16[16,2,48,1536]{3,2,1,0:T(8,128)(2,1)}, u32[]{:S(2)}, u32[]{:S(2)}) async-start(bf16[16,2,48,1536]{3,2,1,0:T(8,128)(2,1)} %bitcast.153), calls=%async_computation.3 | async-start | bytes 9437184 | tf_op jit(solution)/shard_map/all_to_all | solution.py:65
  176.9 2.8 copy.43
  179.7 0.3 copy-done.9
  179.9 1.5 fusion.15
  181.4 1.6 copy-done.10
  183.0 1.4 fusion.1
  184.5 1.5 fusion.16
  186.0 0.8 copy-done.12
  186.8 1.4 fusion.2
  188.2 2.6 maximum_bitcast_fusion
  190.8 9.3 %copy.45 = bf16[1,2,768,1536]{3,1,0,2:T(2,128)(2,1)} copy(bf16[1,2,768,1536]{3,2,1,0:T(8,128)(2,1)} %maximum_bitcast_fusion) | data formatting | bytes 9437184 | tf_op jit(solution)/shard_map/broadcast_in_dim | solution.py:84
  200.1 80.0 %all-to-all-done.3 = bf16[16,2,48,1536]{3,2,1,0:T(8,128)(2,1)} async-done(((bf16[16,2,48,1536]{3,2,1,0:T(8,128)(2,1)}), bf16[16,2,48,1536]{3,2,1,0:T(8,128)(2,1)}, u32[]{:S(2)}, u32[]{:S(2)}) %all-to-all-start.3) | async-done | bytes 4718624 | tf_op jit(solution)/shard_map/all_to_all | solution.py:65
  280.2 5.1 %all-to-all-start.2 = ((bf16[1,2,768,1536]{3,1,0,2:T(2,128)(2,1)}), bf16[1,2,768,1536]{3,1,0,2:T(2,128)(2,1)}, u32[]{:S(2)}, u32[]{:S(2)}) async-start(bf16[1,2,768,1536]{3,1,0,2:T(2,128)(2,1)} %copy.45), calls=%async_computation.2 | async-start | bytes 9437184 | tf_op jit(solution)/shard_map/all_to_all | solution.py:85
  285.4 0.1 copy.40
  285.5 2.6 copy.47
  288.2 1.4 fusion.3
  289.6 0.7 copy-done.4
  290.3 2.4 fusion.4
  292.7 6.2 %fusion.5 = bf16[1,384,1536]{2,1,0:T(8,128)(2,1)} fusion(bf16[1,2,768,1536]{3,2,1,0:T(8,128)(2,1)} %bitcast.158, bf16[1,2,768,1536]{3,2,1,0:T(8,128)(2,1)} %bitcast.162, bf16[1,2,1536,384]{3,2,1,0:T(8,128)(2,1)} %param.14, bf16[1,2,768,384]{3,2,1,0:T(8,128)(2,1)S(1)} %bitcast.167), kind=kOutput, calls=%fused_computation.21 | convolution fusion | flops 1814593536 | bytes 7667712 | tf_op jit(solution)/shard_map/dot_general | solution.py:17
  298.9 6.2 %fusion.6 = bf16[1,384,1536]{2,1,0:T(8,128)(2,1)} fusion(bf16[1,2,768,1536]{3,2,1,0:T(8,128)(2,1)} %bitcast.159, bf16[1,2,768,1536]{3,2,1,0:T(8,128)(2,1)} %bitcast.163, bf16[1,2,1536,384]{3,2,1,0:T(8,128)(2,1)} %param.14, bf16[1,2,768,384]{3,2,1,0:T(8,128)(2,1)S(1)} %bitcast.168), kind=kOutput, calls=%fused_computation.22 | convolution fusion | flops 1814593536 | bytes 7667712 | tf_op jit(solution)/shard_map/dot_general | solution.py:17
  305.1 83.6 %all-to-all-done.2 = bf16[1,2,768,1536]{3,1,0,2:T(2,128)(2,1)} async-done(((bf16[1,2,768,1536]{3,1,0,2:T(2,128)(2,1)}), bf16[1,2,768,1536]{3,1,0,2:T(2,128)(2,1)}, u32[]{:S(2)}, u32[]{:S(2)}) %all-to-all-start.2) | async-done | bytes 4718624 | tf_op jit(solution)/shard_map/all_to_all | solution.py:85
  388.6 5.5 %copy.46 = bf16[1,2,16,48,1536]{4,3,1,2,0:T(8,128)(2,1)} copy(bf16[1,2,16,48,1536]{4,1,3,2,0:T(2,128)(2,1)} %bitcast.30) | data formatting | bytes 9437184 | tf_op jit(solution)/shard_map/all_to_all | solution.py:85
  394.1 10.2 %gather_fusion.2 = bf16[1024,1536]{1,0:T(8,128)(2,1)} fusion(bf16[1536,1536]{1,0:T(8,128)(2,1)} %bitcast.152, s32[1024]{0:T(1024)S(1)} %broadcast_clamp_fusion), kind=kCustom, calls=%fused_computation.4 | custom fusion | bytes 6295552 | tf_op jit(solution)/shard_map/jit(_take)/gather | solution.py:87
  404.4 3.7 fusion
  408.1 1.6 collective-permute-start.1
  409.6 1.6 maximum_bitcast_fusion.2
  411.3 1.7 maximum_bitcast_fusion.1
  412.9 6.6 %collective-permute-done.1 = bf16[1,128,1536]{2,1,0:T(8,128)(2,1)S(1)} collective-permute-done((bf16[1,128,1536]{2,1,0:T(8,128)(2,1)S(1)}, bf16[1,128,1536]{2,1,0:T(8,128)(2,1)S(1)}, u32[]{:S(2)}, u32[]{:S(2)}) %collective-permute-start.1) | collective-permute-done | bytes 393248 | tf_op jit(solution)/shard_map/ppermute | solution.py:10
  419.5 0.7 copy.51
  (50 shorter events, 1.3 us)
Async XLA Ops:
  0.6 22.7 %copy-start = (bf16[1,128,8,384]{3,2,1,0:T(8,128)(2,1)S(1)}, bf16[1,128,8,384]{3,2,1,0:T(8,128)(2,1)}, u32[]{:S(2)}) copy-start(bf16[1,128,8,384]{3,2,1,0:T(8,128)(2,1)} %param.11) | copy-start | bytes 2359300
  28.1 7.6 %copy-start.11 = (bf16[1,128,1536]{2,1,0:T(8,128)(2,1)S(1)}, bf16[1,128,1536]{2,1,0:T(8,128)(2,1)}, u32[]{:S(2)}) copy-start(bf16[1,128,1536]{2,1,0:T(8,128)(2,1)} %param.10) | copy-start | bytes 1179652
  29.4 33.7 %all-to-all-start.1 = ((bf16[16,2,48,384]{3,2,1,0:T(8,128)(2,1)}), bf16[16,2,48,384]{3,2,1,0:T(8,128)(2,1)S(1)}, u32[]{:S(2)}, u32[]{:S(2)}) async-start(bf16[16,2,48,384]{3,2,1,0:T(8,128)(2,1)} %broadcast_select_fusion.1), calls=%async_computation.1 | async-start | bytes 2359296 | tf_op jit(solution)/shard_map/all_to_all | solution.py:66
  35.6 11.2 %collective-permute-start = (bf16[1,128,1536]{2,1,0:T(8,128)(2,1)S(1)}, bf16[1,128,1536]{2,1,0:T(8,128)(2,1)S(1)}, u32[]{:S(2)}, u32[]{:S(2)}) collective-permute-start(bf16[1,128,1536]{2,1,0:T(8,128)(2,1)S(1)} %copy-done.11), channel_id=1, source_target_pairs={{16,0},{0,16},{17,1},{1,17},{18,2},{2,18},{19,3},{3,19},{20,4},{4,... | collective-permute-start | bytes 1179656 | tf_op jit(solution)/shard_map/ppermute | solution.py:10
  63.1 5.2 %copy-start.2 = (bf16[1,128,1536]{2,1,0:T(8,128)(2,1)S(1)}, bf16[1,128,1536]{2,1,0:T(8,128)(2,1)}, u32[]{:S(2)}) copy-start(bf16[1,128,1536]{2,1,0:T(8,128)(2,1)} %param.9) | copy-start | bytes 1179652
  63.1 108.6 %all-to-all-start = ((bf16[16,2,48,1536]{3,2,1,0:T(8,128)(2,1)}), bf16[16,2,48,1536]{3,2,1,0:T(8,128)(2,1)}, u32[]{:S(2)}, u32[]{:S(2)}) async-start(bf16[16,2,48,1536]{3,2,1,0:T(8,128)(2,1)} %bitcast.154), calls=%async_computation | async-start | bytes 9437184 | tf_op jit(solution)/shard_map/all_to_all | solution.py:67
  171.7 108.5 %all-to-all-start.3 = ((bf16[16,2,48,1536]{3,2,1,0:T(8,128)(2,1)}), bf16[16,2,48,1536]{3,2,1,0:T(8,128)(2,1)}, u32[]{:S(2)}, u32[]{:S(2)}) async-start(bf16[16,2,48,1536]{3,2,1,0:T(8,128)(2,1)} %bitcast.153), calls=%async_computation.3 | async-start | bytes 9437184 | tf_op jit(solution)/shard_map/all_to_all | solution.py:65
  176.9 3.1 copy-start.9
  179.7 4.8 %copy-start.3 = (bf16[16,2,48,1536]{3,2,0,1:T(8,128)(2,1)}, bf16[16,2,48,1536]{3,2,0,1:T(8,128)(2,1)S(1)}, u32[]{:S(2)}) copy-start(bf16[16,2,48,1536]{3,2,0,1:T(8,128)(2,1)S(1)} %copy.43) | copy-start | bytes 14155780
  179.9 3.1 copy-start.10
  185.9 0.8 copy-start.12
  200.1 85.2 %copy-start.8 = (s32[1,128,8]{1,2,0:T(8,128)S(1)}, s32[1,128,8]{1,2,0:T(8,128)}, u32[]{:S(2)}) copy-start(s32[1,128,8]{1,2,0:T(8,128)} %param.12) | copy-start | bytes 12292
  280.2 108.5 %all-to-all-start.2 = ((bf16[1,2,768,1536]{3,1,0,2:T(2,128)(2,1)}), bf16[1,2,768,1536]{3,1,0,2:T(2,128)(2,1)}, u32[]{:S(2)}, u32[]{:S(2)}) async-start(bf16[1,2,768,1536]{3,1,0,2:T(2,128)(2,1)} %copy.45), calls=%async_computation.2 | async-start | bytes 9437184 | tf_op jit(solution)/shard_map/all_to_all | solution.py:85
  288.2 2.1 copy-start.4
  288.2 2.1 copy-start.13
  404.4 5.3 %copy-start.6 = (bf16[1,384,1536]{2,1,0:T(8,128)(2,1)S(1)}, bf16[1,384,1536]{2,1,0:T(8,128)(2,1)}, u32[]{:S(2)}) copy-start(bf16[1,384,1536]{2,1,0:T(8,128)(2,1)} %fusion.5) | copy-start | bytes 3538948
  404.4 5.3 %copy-start.7 = (bf16[1,384,1536]{2,1,0:T(8,128)(2,1)S(1)}, bf16[1,384,1536]{2,1,0:T(8,128)(2,1)}, u32[]{:S(2)}) copy-start(bf16[1,384,1536]{2,1,0:T(8,128)(2,1)} %fusion.6) | copy-start | bytes 3538948
  408.0 3.2 copy-start.5
  408.1 11.5 %collective-permute-start.1 = (bf16[1,128,1536]{2,1,0:T(8,128)(2,1)S(1)}, bf16[1,128,1536]{2,1,0:T(8,128)(2,1)S(1)}, u32[]{:S(2)}, u32[]{:S(2)}) collective-permute-start(bf16[1,128,1536]{2,1,0:T(8,128)(2,1)S(1)} %bitcast.170), channel_id=1, source_target_pairs={{16,0},{0,16},{17,1},{1,17},{18,2},{2,18},{19,3},{3,19},{20,4},{4,... | collective-permute-start | bytes 1179656 | tf_op jit(solution)/shard_map/ppermute | solution.py:10
  409.6 10.6 %copy-start.1 = (bf16[1,128,8,384]{3,2,1,0:T(8,128)(2,1)S(1)}, bf16[1,128,8,384]{3,2,1,0:T(8,128)(2,1)}, u32[]{:S(2)}) copy-start(bf16[1,128,8,384]{3,2,1,0:T(8,128)(2,1)} %param.11) | copy-start | bytes 2359300
where the time goes:
time: 421 us; the launch traced here: 420 us
  waiting for transfers between devices  277 us (66%)
  local copies, waits for them, and re-layouts  65 us (15%)
  other arithmetic  30.4 us (7%)
  starting transfers between devices  24.7 us (6%)
  matrix products  22 us (5%)
    all_to_all x1, waiting for transfers between devices, body(): lax.all_to_all(cot_send, 'ep', split_axis=0, concat_axis=2, tiled=True)  92.2 us
    all_to_all x1, waiting for transfers between devices, body(): lax.all_to_all(slot_block, 'ep', split_axis=2, concat_axis=0, tiled=True)  83.6 us
    all_to_all x1, waiting for transfers between devices, body(): lax.all_to_all(x_send, 'ep', split_axis=0, concat_axis=2, tiled=True)  80 us
    ppermute x2, waiting for transfers between devices, from_behind(): return lax.ppermute(block, axis, route)  16.2 us
    dot_general x2, matrix products, expert_grads(): lax.dot_general(hidden, cot_rows, (((0,), (0,)), ((), ())), preferred_ele...  12.3 us
    gather x1, local copies, waits for them, and re-layouts, body(): jnp.take(returned, slot_index, axis=0)  10.2 us
    broadcast_in_dim x1, local copies, waits for them, and re-layouts, body(): slot_block = jnp.stack(slot_grads, axis=0)[None]  9.32 us
    another operation x3, other arithmetic  9.15 us
  transfers between devices with their start and end apart: 6, of which 6 were waited for; matrix products, arithmetic and copies ran while one was open for 15% of the time, Pallas kernels for 0%

commit v1 on v0

v1 whole, which is shorter than its diff:
```python
import jax
import jax.numpy as jnp
from jax import lax
from jax.sharding import PartitionSpec as P

BF16 = jnp.bfloat16
F32 = jnp.float32


def from_behind(block, axis, distance):
    devices = range(lax.axis_size(axis))
    route = [((i - distance) % len(devices), i) for i in devices]
    return lax.ppermute(block, axis, route)


def body(inputs, upstream, gate_saved, expert_ids, route_weights, w_up, w_down):
    ep = lax.axis_size("ep")
    local = w_up.shape[1]
    experts = local * ep
    toks, top = expert_ids.shape[1:]
    cap = 3 * toks * top // (2 * experts)
    width = inputs.shape[2]
    ff = w_up.shape[3]

    routing = jnp.concatenate([expert_ids[0].astype(F32), route_weights[0]], axis=1)
    routing_all = lax.all_gather(routing, "ep", axis=0, tiled=False)

    ids = expert_ids[0]
    hit = ids[:, :, None] == jnp.arange(experts, dtype=jnp.int32)
    member = jnp.any(hit, axis=1).astype(BF16)
    lower = (jnp.arange(toks)[:, None] > jnp.arange(toks)[None, :]).astype(BF16)
    rank = jnp.dot(lower, member, preferred_element_type=F32)
    place = jnp.sum(jnp.where(hit, rank[:, None, :], 0.0), axis=2)
    slot = (ids * cap + place.astype(jnp.int32)).reshape(1, toks * top)
    pick = (jnp.arange(experts * cap, dtype=jnp.int32)[:, None] == slot).astype(BF16)
    gate_send = jnp.dot(pick, gate_saved[0].reshape(toks * top, ff), preferred_element_type=F32)
    gate_send = gate_send.astype(BF16).reshape(ep, local, cap, ff)
    gate_recv = lax.all_to_all(gate_send, "ep", split_axis=0, concat_axis=0, tiled=True)

    cot = from_behind(upstream, "section", -1)[0]
    x_all = lax.all_gather(inputs[0], "ep", axis=0, tiled=True)
    c_all = lax.all_gather(cot, "ep", axis=0, tiled=True)

    me = lax.axis_index("ep")
    mine = (me * local + jnp.arange(local)).astype(F32)
    hits = routing_all[:, :, :top, None] == mine
    weight = jnp.sum(jnp.where(hits, routing_all[:, :, top:, None], 0.0), axis=2)
    members = jnp.any(hits, axis=2)
    ranks = jnp.einsum("ab,sbe->sae", lower, members.astype(BF16), preferred_element_type=F32)
    ranks = jnp.where(members, ranks, -1.0)
    spread = (ranks[:, :, :, None] == jnp.arange(cap).astype(F32)).astype(BF16)
    gate = jnp.einsum("stec,secf->stef", spread, gate_recv, preferred_element_type=F32)
    act = jax.nn.silu(gate).reshape(ep * toks, local, ff)
    weight = weight.reshape(ep * toks, local, 1)
    act_w = (act * weight)

    up = w_up[0]
    down = w_down[0]
    up_cat = jnp.transpose(up, (1, 0, 2)).reshape(width, local * ff)
    down_cat = down.reshape(local * ff, width)
    act_w = act_w.reshape(ep * toks, local * ff)
    u = jnp.dot(x_all, up_cat, preferred_element_type=F32)
    hidden = (act_w * u).astype(BF16)
    h = lax.dot_general(c_all, down_cat, (((1,), (1,)), ((), ())), preferred_element_type=F32)
    g = (act_w * h).astype(BF16)
    part = lax.dot_general(g, up_cat, (((1,), (1,)), ((), ())), preferred_element_type=F32)
    grad = lax.psum_scatter(part.astype(BF16), "ep", scatter_dimension=0, tiled=True)
    delivered = from_behind(grad[None], "section", -1)
    grad_down = lax.dot_general(hidden, c_all, (((0,), (0,)), ((), ())), preferred_element_type=F32)
    grad_up = jnp.stack([
        lax.dot_general(x_all, g[:, e * ff:(e + 1) * ff], (((0,), (0,)), ((), ())), preferred_element_type=F32)
        for e in range(local)
    ])
    return (
        delivered,
        grad_up.astype(BF16)[None],
        grad_down.astype(BF16).reshape(1, local, ff, width),
    )


def solution(mesh):
    return jax.shard_map(
        body,
        mesh=mesh,
        in_specs=(
            P("section", "ep", None),
            P("section", "ep", None),
            P("section", "ep", None, None),
            P("section", "ep", None),
            P("section", "ep", None),
            P("section", "ep", None, None),
            P("section", "ep", None, None),
        ),
        out_specs=(
            P("section", "ep", None),
            P("section", "ep", None, None),
            P("section", "ep", None, None),
        ),
        check_vma=False,
    )
```

time: 421 us -> 274 us (0.65)
  waiting for transfers between devices: 277 us -> 82.3 us
  blocking collectives: 0 us -> 54.2 us
  matrix products: 22 us -> 69.3 us
  local copies, waits for them, and re-layouts: 65 us -> 37.6 us
  other arithmetic: 30.4 us -> 4 us
  starting transfers between devices: 24.7 us -> 9.41 us
  between operations: 0.94 us -> 13.9 us
    all_to_all x4 -> x1, waiting for transfers between devices: 261 us -> 0.01 us  [body(): lax.all_to_all(gate_send, 'ep', split_axis=0, concat_axis=0, tiled=True)]
    all_gather x0 -> x1, blocking collectives: none -> 54.2 us  [body(): routing_all = lax.all_gather(routing, 'ep', axis=0, tiled=False)]
    reduce_scatter x0 -> x1, waiting for transfers between devices: none -> 51.8 us  [body(): lax.psum_scatter(part.astype(BF16), 'ep', scatter_dimension=0, tiled=True)]
    dot_general x8 -> x9, matrix products: 22 us -> 69.3 us  [the longest x1 30.4 us: body(): lax.dot_general(hidden, c_all, (((0,), (0,)), ((), ())), preferred_elemen...]
    gather x5 -> x0, local copies, waits for them, and re-layouts: 33.3 us -> none  [the longest x1 10.2 us: body(): jnp.take(returned, slot_index, axis=0)]
    all_gather x0 -> x2, waiting for transfers between devices: none -> 20.1 us  [the longest x1 20.1 us: body(): x_all = lax.all_gather(inputs[0], 'ep', axis=0, tiled=True)]
    unnamed x31 -> x22, local copies, waits for them, and re-layouts: 5.81 us -> 21.6 us
    all_to_all x4 -> x1, starting transfers between devices: 21.5 us -> 6.24 us  [body(): lax.all_to_all(gate_send, 'ep', split_axis=0, concat_axis=0, tiled=True)]
  transfers between devices with their start and end apart: 6 -> 6, of which waited for: 6 -> 3; matrix products, arithmetic and copies ran while one was open for 15% -> 39% of each run, Pallas kernels for 0% -> 0%
where the time goes in v1:
time: 274 us; the launch traced here: 271 us
  waiting for transfers between devices  82.3 us (30%)
  matrix products  69.3 us (25%)
  blocking collectives  54.2 us (20%)
  local copies, waits for them, and re-layouts  37.6 us (14%)
  between operations  13.9 us (5%)
  starting transfers between devices  9.41 us (3%)
  other arithmetic  4 us (1%)
    all_gather x1, blocking collectives, body(): routing_all = lax.all_gather(routing, 'ep', axis=0, tiled=False)  54.2 us
    reduce_scatter x1, waiting for transfers between devices, body(): lax.psum_scatter(part.astype(BF16), 'ep', scatter_dimension=0, tiled=True)  51.8 us
    dot_general x1, matrix products, body(): lax.dot_general(hidden, c_all, (((0,), (0,)), ((), ())), preferred_elemen...  30.4 us
    unnamed x22, local copies, waits for them, and re-layouts  21.6 us
    all_gather x1, waiting for transfers between devices, body(): x_all = lax.all_gather(inputs[0], 'ep', axis=0, tiled=True)  20.1 us
    dot_general x2, matrix products, body(): lax.dot_general(x_all, g[:, e * ff:(e + 1) * ff], (((0,), (0,)), ((), ())...  11.8 us
    reshape x1, local copies, waits for them, and re-layouts, body(): act = jax.nn.silu(gate).reshape(ep * toks, local, ff)  10.4 us
    dot_general x1, matrix products, body(): lax.dot_general(c_all, down_cat, (((1,), (1,)), ((), ())), preferred_elem...  10.2 us
  transfers between devices with their start and end apart: 6, of which 3 were waited for; matrix products, arithmetic and copies ran while one was open for 39% of the time, Pallas kernels for 0%

profile of v1, /device:TPU:10, one launch (start us, length us, event | category | flops | bytes accessed | tf_op | source)
XLA Modules:
  0.0 270.7 jit_solution(5686237098454286970)
XLA Ops:
  7.2 0.0 copy-start
  7.2 0.0 all-gather.6.cloned.1.call-start
  7.2 1.6 collective-permute-start
  8.8 9.5 %collective-permute-done = bf16[1,128,1536]{2,1,0:T(8,128)(2,1)S(1)} collective-permute-done((bf16[1,128,1536]{2,1,0:T(8,128)(2,1)}, bf16[1,128,1536]{2,1,0:T(8,128)(2,1)S(1)}, u32[]{:S(2)}, u32[]{:S(2)}) %collective-permute-start) | collective-permute-done | bytes 393248 | tf_op jit(solution)/shard_map/ppermute | solution.py:13
  18.4 0.7 copy-done.4
  19.1 0.0 all-gather.6.cloned.1.call-update
  19.1 0.0 all-gather.8.cloned.1.call-start
  19.2 0.7 all-gather.8.cloned.1.call-update
  19.9 0.7 bitcast_convert_fusion
  20.6 0.1 copy.35
  20.7 0.1 mul.41
  20.8 0.7 fusion.45
  21.5 0.1 fusion.47
  21.6 0.7 select_reduce_fusion
  22.4 0.1 copy.36
  22.5 0.1 convert_element_type.56
  22.6 0.0 copy-start.5
  22.6 4.0 %fusion.22 = bf16[1536,384]{1,0:T(8,128)(2,1)} fusion(s32[1024]{0:T(1024)S(1)} %add.23, bf16[1,128,8,384]{3,2,1,0:T(8,128)(2,1)} %param.9), kind=kOutput, calls=%fused_computation.22 | convolution fusion | flops 1210122240 | bytes 1970176 | tf_op jit(solution)/shard_map/dot_general | solution.py:36
  26.5 6.2 %all-to-all-start = ((bf16[16,2,48,384]{3,2,1,0:T(8,128)(2,1)}), bf16[16,2,48,384]{3,2,1,0:T(8,128)(2,1)}, u32[]{:S(2)}, u32[]{:S(2)}) async-start(bf16[16,2,48,384]{3,2,1,0:T(8,128)(2,1)} %bitcast.2), calls=%async_computation | async-start | bytes 2359296 | tf_op jit(solution)/shard_map/all_to_all | solution.py:38
  32.8 0.0 reduce-scatter.2.cloned.1.call-start
  32.8 54.2 %all-gather = f32[2048,16]{0,1:T(8,128)S(1)} all-gather(f32[128,16]{0,1:T(8,128)S(1)} %pad_maximum_fusion.1), channel_id=2, replica_groups=mesh['section'=2,'ep'=16] {'ep'}, dimensions={0}, use_global_device_ids=true | all-gather | bytes 139264 | tf_op jit(solution)/shard_map/all_gather | solution.py:26
  87.1 0.1 compare_reduce_fusion
  87.2 0.1 fusion.37
  87.4 0.1 fusion.44
  87.6 0.4 copy.43
  87.9 4.8 %mul.45 = f32[2048,2,384]{2,1,0:T(2,128)S(1)} broadcast(f32[2048,2]{1,0:T(8,128)S(1)} %copy.43), dimensions={0,1} | broadcast | bytes 6307840 | tf_op jit(solution)/shard_map/mul | solution.py:55
  92.8 3.0 %copy.53 = f32[256,8,2,384]{3,1,2,0:T(8,128)} copy(f32[256,8,2,384]{3,2,1,0:T(2,128)S(1)} %bitcast.86) | data formatting | bytes 12582912
  95.8 4.3 %copy.45 = bf16[1,2,1536,384]{2,3,1,0:T(8,128)(2,1)} copy(bf16[1,2,1536,384]{3,2,1,0:T(8,128)(2,1)} %param.12) | data formatting | bytes 4718592 | tf_op args[5]
  100.1 0.0 all-to-all-done
  100.1 5.8 %bitcast_multiply_fusion = f32[16,128,2,384]{1,3,2,0:T(8,128)} fusion(bf16[16,2,48,384]{3,2,1,0:T(8,128)(2,1)} %all-to-all-done, f32[16,128,2]{1,2,0:T(2,128)S(1)} %copy.40, f32[48]{0:T(128)S(1)} %iota_convert_fusion), kind=kOutput, calls=%fused_computation.11 | convolution fusion | flops 157483008 | bytes 7487680 | tf_op jit(solution)/shard_map/stec,secf->stef/dot_general | solution.py:52
  105.8 10.4 %copy.47 = f32[16,128,2,384]{3,2,1,0:T(2,128)} copy(f32[16,128,2,384]{1,3,2,0:T(8,128)} %bitcast_multiply_fusion) | data formatting | bytes 12582912 | tf_op jit(solution)/shard_map/reshape | solution.py:53
  116.2 5.8 %copy.52 = f32[256,8,2,384]{3,1,2,0:T(8,128)} copy(f32[256,8,2,384]{3,2,1,0:T(2,128)} %bitcast.87) | data formatting | bytes 12582912
  122.0 10.2 %multiply_convert_fusion.1 = bf16[2048,768]{1,0:T(8,128)(2,1)S(1)} fusion(bf16[768,1536]{1,0:T(8,128)(2,1)S(1)} %bitcast.85, bf16[1,2048,1536]{2,1,0:T(8,128)(2,1)} %all-gather.6.cloned.1.call-done, f32[2048,768]{1,0:T(8,128)} %bitcast.90, f32[2048,768]{1,0:T(8,128)} %bitcast.88), kind=kOutput, calls=%fused_computation.17 | convolution fusion | flops 4836556800 | bytes 24379392 | tf_op jit(solution)/shard_map/dot_general | solution.py:64
  132.2 1.6 copy-done.6
  133.8 6.9 %convolution_convert_fusion = bf16[2048,1536]{1,0:T(8,128)(2,1)} fusion(bf16[2048,768]{1,0:T(8,128)(2,1)S(1)} %multiply_convert_fusion.1, bf16[1536,768]{0,1:T(8,128)(2,1)S(1)} %bitcast.92), kind=kOutput, calls=%fused_computation | convolution fusion | flops 4834983936 | bytes 11796480 | tf_op jit(solution)/shard_map/dot_general | solution.py:66
  140.8 0.0 reduce-scatter.2.cloned.1.call-update
  140.8 0.0 copy-start.3
  140.8 20.1 %all-gather.8.cloned.1.call-done = bf16[1,2048,1536]{2,1,0:T(8,128)(2,1)} async-done(((bf16[1,128,1536]{2,1,0:T(8,128)(2,1)}), bf16[1,2048,1536]{2,1,0:T(8,128)(2,1)}) %all-gather.8.cloned.1.call-update) | async-done | bytes 6291472 | tf_op jit(solution)/shard_map/all_gather | solution.py:41
  160.9 5.9 %fusion.29 = bf16[1,1,1536,384]{2,3,1,0:T(8,128)(2,1)S(1)} fusion(bf16[1,2048,1536]{2,1,0:T(8,128)(2,1)} %all-gather.8.cloned.1.call-done, bf16[2048,768]{1,0:T(8,128)(2,1)} %copy-done.6), kind=kOutput, calls=%fused_computation.25 | convolution fusion | flops 2416508928 | bytes 9043968 | tf_op jit(solution)/shard_map/dot_general | solution.py:71
  166.9 30.4 %fusion.18 = bf16[768,1536]{1,0:T(8,128)(2,1)} fusion(bf16[1,2048,1536]{2,1,0:T(8,128)(2,1)} %all-gather.6.cloned.1.call-done, bf16[1536,768]{0,1:T(8,128)(2,1)S(1)} %bitcast.93, bf16[1,2048,1536]{2,1,0:T(8,128)(2,1)} %all-gather.8.cloned.1.call-done, f32[2048,768]{1,0:T(8,128)} %bitcast.91, f32[2048,768]{1,0:T(8,128)} %bitcast.89), kind=kOutput, calls=%fused_computation.20 | convolution fusion | flops 9669574656 | bytes 29884416 | tf_op jit(solution)/shard_map/dot_general | solution.py:69
  197.3 51.8 %reduce-scatter.2.cloned.1.call-done = bf16[128,1536]{1,0:T(8,128)(2,1)} async-done(((bf16[2048,1536]{1,0:T(8,128)(2,1)}), bf16[128,1536]{1,0:T(8,128)(2,1)}) %reduce-scatter.2.cloned.1.call-update) | async-done | bytes 393232 | tf_op jit(solution)/shard_map/reduce_scatter | solution.py:67
  249.1 1.5 collective-permute-start.1
  250.6 5.9 %fusion.32 = bf16[1,1,1536,384]{2,3,1,0:T(8,128)(2,1)S(1)} fusion(bf16[1,2048,1536]{2,1,0:T(8,128)(2,1)} %all-gather.8.cloned.1.call-done, bf16[2048,768]{1,0:T(8,128)(2,1)} %copy-done.6), kind=kOutput, calls=%fused_computation.26 | convolution fusion | flops 2416508928 | bytes 9043968 | tf_op jit(solution)/shard_map/dot_general | solution.py:71
  256.5 0.0 copy-start.1
  256.5 1.6 pad_maximum_fusion
  258.1 4.3 %copy.46 = bf16[1,2,1536,384]{3,2,1,0:T(8,128)(2,1)} copy(bf16[1,2,1536,384]{2,3,1,0:T(8,128)(2,1)} %pad_maximum_fusion) | data formatting | bytes 4718592
  262.4 0.0 collective-permute-done.1
  262.4 1.8 copy.57
  (19 shorter events, 0.1 us)
Async XLA Ops:
  7.2 114.9 %copy-start = (bf16[1,2,384,1536]{3,2,1,0:T(8,128)(2,1)S(1)}, bf16[1,2,384,1536]{3,2,1,0:T(8,128)(2,1)}, u32[]{:S(2)}) copy-start(bf16[1,2,384,1536]{3,2,1,0:T(8,128)(2,1)} %param.13) | copy-start | bytes 7077892
  7.2 114.8 %all-gather.6.cloned.1.call-start = ((), (), s32[]{:S(2)}) async-start(), calls=%async_computation.3 | async-start | bytes 6684672 | tf_op jit(solution)/shard_map/all_gather | solution.py:42
  7.2 11.1 %collective-permute-start = (bf16[1,128,1536]{2,1,0:T(8,128)(2,1)}, bf16[1,128,1536]{2,1,0:T(8,128)(2,1)S(1)}, u32[]{:S(2)}, u32[]{:S(2)}) collective-permute-start(bf16[1,128,1536]{2,1,0:T(8,128)(2,1)} %param.8), channel_id=1, source_target_pairs={{16,0},{0,16},{17,1},{1,17},{18,2},{2,18},{19,3},{3,19},{20,4},{4,... | collective-permute-start | bytes 1179656 | tf_op jit(solution)/shard_map/ppermute | solution.py:13
  18.4 0.7 copy-start.4
  19.1 141.8 %all-gather.8.cloned.1.call-start = ((), (), s32[]{:S(2)}) async-start(), calls=%async_computation.4 | async-start | bytes 6684672 | tf_op jit(solution)/shard_map/all_gather | solution.py:41
  22.6 10.3 %copy-start.5 = (f32[1,128,8]{1,2,0:T(8,128)S(1)}, f32[1,128,8]{1,2,0:T(8,128)}, u32[]{:S(2)}) copy-start(f32[1,128,8]{1,2,0:T(8,128)} %param.11) | copy-start | bytes 12292
  26.5 73.5 %all-to-all-start = ((bf16[16,2,48,384]{3,2,1,0:T(8,128)(2,1)}), bf16[16,2,48,384]{3,2,1,0:T(8,128)(2,1)}, u32[]{:S(2)}, u32[]{:S(2)}) async-start(bf16[16,2,48,384]{3,2,1,0:T(8,128)(2,1)} %bitcast.2), calls=%async_computation | async-start | bytes 2359296 | tf_op jit(solution)/shard_map/all_to_all | solution.py:38
  32.8 216.3 %reduce-scatter.2.cloned.1.call-start = ((), (), s32[]{:S(2)}) async-start(), calls=%async_computation.2 | async-start | bytes 6684672 | tf_op jit(solution)/shard_map/reduce_scatter | solution.py:67
  122.0 11.8 %copy-start.2 = (bf16[1,2,1536,384]{2,3,1,0:T(8,128)(2,1)S(1)}, bf16[1,2,1536,384]{2,3,1,0:T(8,128)(2,1)}, u32[]{:S(2)}) copy-start(bf16[1,2,1536,384]{2,3,1,0:T(8,128)(2,1)} %copy.45) | copy-start | bytes 7077892
  132.2 1.6 copy-start.6
  140.8 26.0 %copy-start.3 = (bf16[1,2,1536,384]{2,3,1,0:T(8,128)(2,1)S(1)}, bf16[1,2,1536,384]{2,3,1,0:T(8,128)(2,1)}, u32[]{:S(2)}) copy-start(bf16[1,2,1536,384]{2,3,1,0:T(8,128)(2,1)} %copy.45) | copy-start | bytes 7077892
  249.1 13.3 %collective-permute-start.1 = (bf16[1,128,1536]{2,1,0:T(8,128)(2,1)}, bf16[1,128,1536]{2,1,0:T(8,128)(2,1)}, u32[]{:S(2)}, u32[]{:S(2)}) collective-permute-start(bf16[1,128,1536]{2,1,0:T(8,128)(2,1)} %bitcast.100), channel_id=1, source_target_pairs={{16,0},{0,16},{17,1},{1,17},{18,2},{2,18},{19,3},{3,19},{20,4},{4,... | collective-permute-start | bytes 1179656 | tf_op jit(solution)/shard_map/ppermute | solution.py:13
  256.5 7.7 %copy-start.1 = (bf16[1,2,384,1536]{3,2,1,0:T(8,128)(2,1)S(1)}, bf16[1,2,384,1536]{3,2,1,0:T(8,128)(2,1)}, u32[]{:S(2)}) copy-start(bf16[1,2,384,1536]{3,2,1,0:T(8,128)(2,1)} %param.13) | copy-start | bytes 7077892
Sparse Core Ops, SparseCore 0:
  19.2 79.0 all-gather.5
  100.6 60.2 all-gather.7
  164.9 84.1 reduce-scatter.1

commit v2 on v1

v2 whole, which is shorter than its diff:
```python
import functools

import jax
import jax.numpy as jnp
from jax import lax
from jax.experimental import pallas as pl
from jax.experimental.pallas import tpu as pltpu
from jax.sharding import PartitionSpec as P

BF16 = jnp.bfloat16
F32 = jnp.float32


def from_behind(block, axis, distance):
    devices = range(lax.axis_size(axis))
    route = [((i - distance) % len(devices), i) for i in devices]
    return lax.ppermute(block, axis, route)


def gather_kernel(grid, sections, x_ref, u_ref, x_out, c_out, own_sem, shift_send, send_sem, recv_sem, pair_recv):
    outer, inner, pair = grid
    me = lax.axis_index("ep")
    sec = lax.axis_index("section")
    core = lax.rem(me, pair)
    here = (lax.div(me, inner * pair), lax.rem(lax.div(me, pair), inner))
    sizes = (outer, inner)
    half = x_ref.shape[0] // 2

    def moved(dim, step):
        spot = list(here)
        spot[dim] = lax.rem(here[dim] + step + sizes[dim], sizes[dim])
        return (spot[0] * inner + spot[1]) * pair + core

    other = me + 1 - 2 * core
    before = lax.rem(sec + sections - 1, sections)
    after = lax.rem(sec + 1, sections)

    barrier = pltpu.get_barrier_semaphore()
    greeted = 0
    for target in [{"section": before}, {"section": after}] + [
        {"ep": d} for d in [other] + [moved(dim, step) for dim in range(2) if sizes[dim] > 1 for step in (1, -1)]
    ]:
        pl.semaphore_signal(barrier, inc=1, device_id=target, device_id_type=pl.DeviceIdType.MESH)
        greeted += 1
    pl.semaphore_wait(barrier, greeted)

    outs = (x_out, c_out)
    orders = ((0, 1), (1, 0))
    pending = []

    def slice_of(a, owner, h):
        return outs[a].at[owner, pl.ds(h * half, half)]

    def own_slice(ref, h):
        return ref.at[pl.ds(h * half, half)]

    for h in range(2):
        cp = pltpu.make_async_remote_copy(
            src_ref=own_slice(u_ref, h), dst_ref=slice_of(1, me, h),
            send_sem=shift_send.at[h], recv_sem=recv_sem.at[1, 0, h],
            device_id={"section": before}, device_id_type=pl.DeviceIdType.MESH)
        cp.start()
        pending.append(cp)
    keep = pltpu.make_async_copy(x_ref, x_out.at[me], own_sem)
    keep.start()

    arrivals = []
    for level in range(outer + inner - 1):
        for a in range(2):
            d1, d2 = orders[a]
            for i in range(sizes[d1]):
                j = level - i
                if j < 0 or j >= sizes[d2]:
                    continue
                for h in range(2):
                    sign = 1 - 2 * h
                    spot = [None, None]
                    spot[d1] = lax.rem(here[d1] - sign * i + sizes[d1], sizes[d1])
                    spot[d2] = lax.rem(here[d2] - sign * j + sizes[d2], sizes[d2])
                    base = (spot[0] * inner + spot[1]) * pair
                    owner = base + core
                    n = i * sizes[d2] + j
                    block = slice_of(a, owner, h)
                    if a == 1 or level > 0:
                        pltpu.make_async_remote_copy(
                            src_ref=block, dst_ref=block, send_sem=send_sem.at[a, n, h, 0],
                            recv_sem=recv_sem.at[a, n, h], device_id={"ep": other},
                            device_id_type=pl.DeviceIdType.MESH).wait_recv()
                    src = own_slice(x_ref, h) if (a == 0 and level == 0) else block
                    hops = []
                    if j == 0 and i < sizes[d1] - 1:
                        hops.append((1, moved(d1, sign), recv_sem.at[a, (i + 1) * sizes[d2], h]))
                    if j < sizes[d2] - 1:
                        hops.append((2, moved(d2, sign), recv_sem.at[a, n + 1, h]))
                    hops.append((0, other, pair_recv.at[a, n, h]))
                    for kind, target, landed in hops:
                        cp = pltpu.make_async_remote_copy(
                            src_ref=src, dst_ref=block, send_sem=send_sem.at[a, n, h, kind],
                            recv_sem=landed, device_id={"ep": target},
                            device_id_type=pl.DeviceIdType.MESH)
                        cp.start()
                        pending.append(cp)
                    arrivals.append((a, n, h, slice_of(a, base + 1 - core, h)))
    for a, n, h, block in arrivals:
        pltpu.make_async_remote_copy(
            src_ref=block, dst_ref=block, send_sem=send_sem.at[a, n, h, 0],
            recv_sem=pair_recv.at[a, n, h], device_id={"ep": other},
            device_id_type=pl.DeviceIdType.MESH).wait_recv()
    for cp in pending:
        cp.wait_send()
    keep.wait()


def gather_tokens(x, u):
    ep = lax.axis_size("ep")
    outer = 4 if ep % 8 == 0 else 1
    grid = (outer, ep // (2 * outer), 2)
    toks, width = x.shape
    spots = ep // 2
    out = jax.ShapeDtypeStruct((ep, toks, width), x.dtype)
    return pl.pallas_call(
        functools.partial(gather_kernel, grid, lax.axis_size("section")),
        out_shape=(out, out),
        in_specs=[pl.BlockSpec(memory_space=pl.ANY)] * 2,
        out_specs=(pl.BlockSpec(memory_space=pl.ANY),) * 2,
        scratch_shapes=[
            pltpu.SemaphoreType.DMA,
            pltpu.SemaphoreType.DMA((2,)),
            pltpu.SemaphoreType.DMA((2, spots, 2, 3)),
            pltpu.SemaphoreType.DMA((2, spots, 2)),
            pltpu.SemaphoreType.DMA((2, spots, 2)),
        ],
        compiler_params=pltpu.CompilerParams(collective_id=0, has_side_effects=True),
        name="gather_tokens",
    )(x, u)


def body(inputs, upstream, gate_saved, expert_ids, route_weights, w_up, w_down):
    ep = lax.axis_size("ep")
    local = w_up.shape[1]
    experts = local * ep
    toks, top = expert_ids.shape[1:]
    cap = 3 * toks * top // (2 * experts)
    width = inputs.shape[2]
    ff = w_up.shape[3]

    routing = jnp.concatenate([expert_ids[0].astype(F32), route_weights[0]], axis=1)
    routing_all = lax.all_gather(routing, "ep", axis=0, tiled=False)

    ids = expert_ids[0]
    hit = ids[:, :, None] == jnp.arange(experts, dtype=jnp.int32)
    member = jnp.any(hit, axis=1).astype(BF16)
    lower = (jnp.arange(toks)[:, None] > jnp.arange(toks)[None, :]).astype(BF16)
    rank = jnp.dot(lower, member, preferred_element_type=F32)
    place = jnp.sum(jnp.where(hit, rank[:, None, :], 0.0), axis=2)
    slot = (ids * cap + place.astype(jnp.int32)).reshape(1, toks * top)
    pick = (jnp.arange(experts * cap, dtype=jnp.int32)[:, None] == slot).astype(BF16)
    gate_send = jnp.dot(pick, gate_saved[0].reshape(toks * top, ff), preferred_element_type=F32)
    gate_send = gate_send.astype(BF16).reshape(ep, local, cap, ff)
    gate_recv = lax.all_to_all(gate_send, "ep", split_axis=0, concat_axis=0, tiled=True)

    x_all, c_all = gather_tokens(inputs[0], upstream[0])
    x_all = x_all.reshape(ep * toks, width)
    c_all = c_all.reshape(ep * toks, width)

    me = lax.axis_index("ep")
    named, weights = routing_all[:, :, :top], routing_all[:, :, top:]
    hiddens, grads = [], []
    for e in range(local):
        hits = named == (me * local + e).astype(F32)
        weight = jnp.sum(jnp.where(hits, weights, 0.0), axis=2)
        here = jnp.any(hits, axis=2)
        rank_here = lax.dot_general(here.astype(BF16), lower, (((1,), (1,)), ((), ())), preferred_element_type=F32)
        rank_here = jnp.where(here, rank_here, -1.0)
        spread = (rank_here[:, :, None] == jnp.arange(cap).astype(F32)).astype(BF16)
        gate = lax.dot_general(
            spread, gate_recv[:, e], (((2,), (1,)), ((0,), (0,))), preferred_element_type=F32
        ).reshape(ep * toks, ff)
        act = jax.nn.silu(gate) * weight.reshape(ep * toks, 1)
        u = jnp.dot(x_all, w_up[0, e], preferred_element_type=F32)
        h = lax.dot_general(c_all, w_down[0, e], (((1,), (1,)), ((), ())), preferred_element_type=F32)
        hiddens.append((act * u).astype(BF16))
        grads.append((act * h).astype(BF16))
    g = jnp.concatenate(grads, axis=1)
    up_cat = jnp.concatenate([w_up[0, e] for e in range(local)], axis=1)
    part = lax.dot_general(g, up_cat, (((1,), (1,)), ((), ())), preferred_element_type=F32)
    grad = lax.psum_scatter(part.astype(BF16), "ep", scatter_dimension=0, tiled=True)
    delivered = from_behind(grad[None], "section", -1)
    over_tokens = (((0,), (0,)), ((), ()))
    grad_up = [lax.dot_general(x_all, r, over_tokens, preferred_element_type=F32).astype(BF16) for r in grads]
    grad_down = [lax.dot_general(r, c_all, over_tokens, preferred_element_type=F32).astype(BF16) for r in hiddens]
    return (delivered, jnp.stack(grad_up)[None], jnp.stack(grad_down)[None])


def solution(mesh):
    return jax.shard_map(
        body,
        mesh=mesh,
        in_specs=(
            P("section", "ep", None),
            P("section", "ep", None),
            P("section", "ep", None, None),
            P("section", "ep", None),
            P("section", "ep", None),
            P("section", "ep", None, None),
            P("section", "ep", None, None),
        ),
        out_specs=(
            P("section", "ep", None),
            P("section", "ep", None, None),
            P("section", "ep", None, None),
        ),
        check_vma=False,
    )
```

time: 274 us -> 283 us (1.033)
  Pallas kernels: 0 us -> 83.3 us
  waiting for transfers between devices: 82.3 us -> 47.3 us
  local copies, waits for them, and re-layouts: 37.6 us -> 13.9 us
  blocking collectives: 54.2 us -> 37.3 us
  other arithmetic: 4 us -> 7.18 us
    pallas_call x0 -> x1, Pallas kernels: none -> 83.3 us  [gather_tokens(): pl.pallas_call(functools.partial(gather_kernel, grid, lax.axis_size('sect...]
    all_gather x2 -> x0, waiting for transfers between devices: 20.1 us -> none  [the longest x1 20.1 us: body(): x_all = lax.all_gather(inputs[0], 'ep', axis=0, tiled=True)]
    unnamed x22 -> x26, local copies, waits for them, and re-layouts: 21.6 us -> 3.33 us
    all_gather x1, blocking collectives: 54.2 us -> 37.3 us  [body(): routing_all = lax.all_gather(routing, 'ep', axis=0, tiled=False)]
    reduce_scatter x1, waiting for transfers between devices: 51.8 us -> 43.2 us  [body(): lax.psum_scatter(part.astype(BF16), 'ep', scatter_dimension=0, tiled=True)]
    ppermute x2 -> x1, waiting for transfers between devices: 9.55 us -> 4.08 us  [from_behind(): return lax.ppermute(block, axis, route)]
    mul x2 -> x0, local copies, waits for them, and re-layouts: 5.21 us -> none  [body(): act_w = act * weight]
    broadcast_in_dim x0 -> x2, other arithmetic: none -> 4.9 us  [body(): return (delivered, jnp.stack(grad_up)[None], jnp.stack(grad_down)[None])]
  transfers between devices with their start and end apart: 6 -> 3, of which waited for: 3 -> 2; matrix products, arithmetic and copies ran while one was open for 39% -> 18% of each run, Pallas kernels for 0% -> 30%
where the time goes in v2:
time: 283 us; the launch traced here: 281 us
  Pallas kernels  83.3 us (29%)
  matrix products  69.6 us (25%)
  waiting for transfers between devices  47.3 us (17%)
  blocking collectives  37.3 us (13%)
  between operations  14.2 us (5%)
  local copies, waits for them, and re-layouts  13.9 us (5%)
  starting transfers between devices  7.75 us (3%)
  other arithmetic  7.18 us (3%)
    pallas_call x1, Pallas kernels, gather_tokens(): pl.pallas_call(functools.partial(gather_kernel, grid, lax.axis_size('sect...  83.3 us
    reduce_scatter x1, waiting for transfers between devices, body(): lax.psum_scatter(part.astype(BF16), 'ep', scatter_dimension=0, tiled=True)  43.2 us
    all_gather x1, blocking collectives, body(): routing_all = lax.all_gather(routing, 'ep', axis=0, tiled=False)  37.3 us
    dot_general x2, matrix products, body(): lax.dot_general(r, c_all, over_tokens, preferred_element_type=F32)  25.8 us
    dot_general x2, matrix products, body(): lax.dot_general(x_all, r, over_tokens, preferred_element_type=F32)  15.4 us
    dot_general x2, matrix products, body(): lax.dot_general(c_all, w_down[0, e], (((1,), (1,)), ((), ())), preferred_...  13.2 us
    dot_general x1, matrix products, body(): lax.dot_general(g, up_cat, (((1,), (1,)), ((), ())), preferred_element_ty...  7.33 us
    reshape x2, local copies, waits for them, and re-layouts, body(): gate = lax.dot_general(spread, gate_recv[:, e], (((2,), (1,)), ((0,), (0,...  7.28 us
  transfers between devices with their start and end apart: 3, of which 2 were waited for; matrix products, arithmetic and copies ran while one was open for 18% of the time, Pallas kernels for 30%

profile of v2, /device:TPU:10, one launch (start us, length us, event | category | flops | bytes accessed | tf_op | source)
XLA Modules:
  0.0 280.5 jit_solution(2964931750582867920)
XLA Ops:
  7.2 0.0 copy-start
  7.2 0.8 broadcast_multiply_fusion
  7.9 0.7 fusion.26
  8.7 0.1 fusion.27
  8.8 0.7 select_reduce_fusion
  9.5 0.1 copy.34
  9.6 0.1 convert_element_type.70
  9.7 0.1 copy.33
  9.8 0.1 mul.59
  9.9 0.0 copy-done
  9.9 0.0 copy-start.6
  10.0 2.8 %fusion.5 = bf16[1536,384]{1,0:T(8,128)(2,1)} fusion(s32[1024]{0:T(1024)S(1)} %add.19, bf16[1,128,8,384]{3,2,1,0:T(8,128)(2,1)S(1)} %copy-done), kind=kOutput, calls=%fused_computation.13 | convolution fusion | flops 1210122240 | bytes 1970176 | tf_op jit(solution)/shard_map/dot_general | solution.py:158
  12.8 6.2 %all-to-all-start = ((bf16[16,2,48,384]{3,2,1,0:T(8,128)(2,1)}), bf16[16,2,48,384]{3,2,1,0:T(8,128)(2,1)S(1)}, u32[]{:S(2)}, u32[]{:S(2)}) async-start(bf16[16,2,48,384]{3,2,1,0:T(8,128)(2,1)} %bitcast.3), calls=%async_computation | async-start | bytes 2359296 | tf_op jit(solution)/shard_map/all_to_all | solution.py:160
  19.0 0.0 reduce-scatter.2.cloned.1.call-start
  19.1 0.0 copy-done.6
  19.1 37.3 %all-gather = f32[2048,16]{0,1:T(8,128)S(1)} all-gather(f32[128,16]{0,1:T(8,128)S(1)} %pad_maximum_fusion), channel_id=2, replica_groups=mesh['section'=2,'ep'=16] {'ep'}, dimensions={0}, use_global_device_ids=true | all-gather | bytes 139264 | tf_op jit(solution)/shard_map/all_gather | solution.py:148
  56.4 83.3 %gather_tokens.1 = (bf16[16,128,1536]{2,1,0:T(8,128)(2,1)}, bf16[16,128,1536]{2,1,0:T(8,128)(2,1)}) custom-call(bf16[128,1536]{1,0:T(8,128)(2,1)} %bitcast.74, bf16[128,1536]{1,0:T(8,128)(2,1)} %bitcast.75), custom_call_target="tpu_custom_call" | custom-call | tf_op jit(solution)/shard_map/gather_tokens/pallas_call | solution.py:121
  139.8 0.1 convolution_select_fusion
  139.9 0.2 convolution_select_fusion.1
  140.1 2.9 %slice_bitcast_fusion.1 = (bf16[1536,384]{1,0:T(8,128)(2,1)S(1)}, bf16[1536,384]{1,0:T(8,128)(2,1)}) fusion(bf16[1,2,1536,384]{3,2,1,0:T(8,128)(2,1)} %param.12), kind=kLoop, calls=%fused_computation.30 | loop fusion | bytes 4718592 | tf_op jit(solution)/shard_map/squeeze | solution.py:185
  143.0 0.0 all-to-all-done
  143.0 2.4 fusion.19
  145.3 3.6 %copy.37 = f32[2048,384]{0,1:T(8,128)} copy(f32[2048,384]{1,0:T(8,128)} %bitcast.70) | data formatting | bytes 6291456 | tf_op jit(solution)/shard_map/reshape | solution.py:178
  148.9 2.4 fusion.18
  151.3 3.7 %copy.44 = f32[2048,384]{0,1:T(8,128)} copy(f32[2048,384]{1,0:T(8,128)} %bitcast.69) | data formatting | bytes 6291456 | tf_op jit(solution)/shard_map/reshape | solution.py:178
  155.0 6.9 %multiply_convert_fusion.2 = bf16[2048,384]{0,1:T(8,128)(2,1)S(1)} fusion(bf16[2048,1536]{1,0:T(8,128)(2,1)} %bitcast.87, bf16[1,2,384,1536]{3,2,1,0:T(8,128)(2,1)} %param.13, f32[2048]{0:T(1024)S(1)} %bitcast.80, f32[2048,384]{0,1:T(8,128)} %copy.44), kind=kOutput, calls=%fused_computation.8 | convolution fusion | flops 2421424128 | bytes 12197888 | tf_op jit(solution)/shard_map/dot_general | solution.py:181
  161.9 0.0 copy-start.8
  161.9 0.0 copy-done.1
  161.9 0.0 copy-done.7
  161.9 0.0 copy-start.3
  161.9 6.3 %multiply_convert_fusion.3 = bf16[2048,384]{0,1:T(8,128)(2,1)S(1)} fusion(bf16[2048,1536]{1,0:T(8,128)(2,1)} %bitcast.88, bf16[1,2,384,1536]{3,2,1,0:T(8,128)(2,1)S(1)} %copy-done.7, f32[2048]{0:T(1024)S(1)} %bitcast.78, f32[2048,384]{0,1:T(8,128)S(1)} %copy-done.1), kind=kOutput, calls=%fused_computation.10 | convolution fusion | flops 2421424128 | bytes 12197888 | tf_op jit(solution)/shard_map/dot_general | solution.py:181
  168.2 0.0 copy-start.10
  168.2 0.0 copy-done.8
  168.2 1.1 copy-done.10
  169.3 0.0 copy-done.3
  169.3 7.3 %convolution_convert_fusion = bf16[2048,1536]{1,0:T(8,128)(2,1)} fusion(bf16[2048,384]{0,1:T(8,128)(2,1)S(1)} %multiply_convert_fusion.2, bf16[2048,384]{0,1:T(8,128)(2,1)S(1)} %multiply_convert_fusion.3, bf16[1536,384]{1,0:T(8,128)(2,1)S(1)} %copy-done.3, bf16[1536,384]{1,0:T(8,128)(2,1)S(1)} %get-tuple-element.13), kind=kOutput, calls=%fused_computation | convolution fusion | flops 4845993984 | bytes 11796480 | tf_op jit(solution)/shard_map/dot_general | solution.py:186
  176.7 0.0 reduce-scatter.2.cloned.1.call-update
  176.7 1.4 copy-done.9
  178.1 7.4 %fusion.7 = bf16[1,1536,384]{2,1,0:T(8,128)(2,1)} fusion(bf16[2048,1536]{1,0:T(8,128)(2,1)} %bitcast.83, bf16[2048,384]{0,1:T(8,128)(2,1)S(1)} %copy-done.9), kind=kOutput, calls=%fused_computation.19 | convolution fusion | flops 2416508928 | bytes 9043968 | tf_op jit(solution)/shard_map/dot_general | solution.py:190
  185.5 8.0 %fusion.6 = bf16[1,1536,384]{2,1,0:T(8,128)(2,1)} fusion(bf16[2048,1536]{1,0:T(8,128)(2,1)} %bitcast.84, bf16[2048,384]{0,1:T(8,128)(2,1)S(1)} %copy-done.11), kind=kOutput, calls=%fused_computation.18 | convolution fusion | flops 2416508928 | bytes 9043968 | tf_op jit(solution)/shard_map/dot_general | solution.py:190
  193.5 12.8 %fusion.9 = bf16[1,384,1536]{2,1,0:T(8,128)(2,1)} fusion(bf16[2048,1536]{1,0:T(8,128)(2,1)} %bitcast.89, bf16[2048,1536]{1,0:T(8,128)(2,1)} %bitcast.85, f32[2048,384]{0,1:T(8,128)} %copy.44, f32[2048]{0:T(1024)S(1)} %bitcast.81, bf16[1,2,1536,384]{3,2,1,0:T(8,128)(2,1)S(1)} %copy-done.2), kind=kOutput, calls=%fused_computation.21 | convolution fusion | flops 4837933056 | bytes 18096128 | tf_op jit(solution)/shard_map/dot_general | solution.py:191
  206.3 12.9 %fusion.8 = bf16[1,384,1536]{2,1,0:T(8,128)(2,1)} fusion(bf16[2048,1536]{1,0:T(8,128)(2,1)} %bitcast.90, bf16[2048,1536]{1,0:T(8,128)(2,1)} %bitcast.86, f32[2048,384]{0,1:T(8,128)} %copy.37, f32[2048]{0:T(1024)S(1)} %bitcast.79, bf16[1,2,1536,384]{3,2,1,0:T(8,128)(2,1)S(1)} %copy-done.2), kind=kOutput, calls=%fused_computation.20 | convolution fusion | flops 4837933056 | bytes 18096128 | tf_op jit(solution)/shard_map/dot_general | solution.py:191
  219.3 43.2 %reduce-scatter.2.cloned.1.call-done = bf16[128,1536]{1,0:T(8,128)(2,1)} async-done(((bf16[2048,1536]{1,0:T(8,128)(2,1)}), bf16[128,1536]{1,0:T(8,128)(2,1)}) %reduce-scatter.2.cloned.1.call-update) | async-done | bytes 393232 | tf_op jit(solution)/shard_map/reduce_scatter | solution.py:187
  262.5 1.5 collective-permute-start
  264.0 3.3 %maximum_bitcast_fusion = bf16[1,2,1536,384]{3,2,1,0:T(8,128)(2,1)} fusion(bf16[1,1536,384]{2,1,0:T(8,128)(2,1)} %fusion.7, bf16[1,1536,384]{2,1,0:T(8,128)(2,1)} %fusion.6), kind=kLoop, calls=%fused_computation.25 | loop fusion | flops 1179648 | bytes 4718592 | tf_op jit(solution)/shard_map/broadcast_in_dim | solution.py:192
  267.3 1.6 maximum_bitcast_fusion.1
  268.9 4.1 %collective-permute-done = bf16[1,128,1536]{2,1,0:T(8,128)(2,1)S(1)} collective-permute-done((bf16[1,128,1536]{2,1,0:T(8,128)(2,1)}, bf16[1,128,1536]{2,1,0:T(8,128)(2,1)S(1)}, u32[]{:S(2)}, u32[]{:S(2)}) %collective-permute-start) | collective-permute-done | bytes 393248 | tf_op jit(solution)/shard_map/ppermute | solution.py:17
  273.0 0.7 copy.49
  (18 shorter events, 0.1 us)
Async XLA Ops:
  7.2 2.8 copy-start
  9.9 9.1 %copy-start.6 = (f32[1,128,8]{1,2,0:T(8,128)S(1)}, f32[1,128,8]{1,2,0:T(8,128)}, u32[]{:S(2)}) copy-start(f32[1,128,8]{1,2,0:T(8,128)} %param.11) | copy-start | bytes 12292
  12.8 130.2 %all-to-all-start = ((bf16[16,2,48,384]{3,2,1,0:T(8,128)(2,1)}), bf16[16,2,48,384]{3,2,1,0:T(8,128)(2,1)S(1)}, u32[]{:S(2)}, u32[]{:S(2)}) async-start(bf16[16,2,48,384]{3,2,1,0:T(8,128)(2,1)} %bitcast.3), calls=%async_computation | async-start | bytes 2359296 | tf_op jit(solution)/shard_map/all_to_all | solution.py:160
  19.0 243.5 %reduce-scatter.2.cloned.1.call-start = ((), (), s32[]{:S(2)}) async-start(), calls=%async_computation.2 | async-start | bytes 6684672 | tf_op jit(solution)/shard_map/reduce_scatter | solution.py:187
  155.0 6.9 %copy-start.1 = (f32[2048,384]{0,1:T(8,128)S(1)}, f32[2048,384]{0,1:T(8,128)}, u32[]{:S(2)}) copy-start(f32[2048,384]{0,1:T(8,128)} %copy.37) | copy-start | bytes 9437188
  155.0 6.9 %copy-start.7 = (bf16[1,2,384,1536]{3,2,1,0:T(8,128)(2,1)S(1)}, bf16[1,2,384,1536]{3,2,1,0:T(8,128)(2,1)}, u32[]{:S(2)}) copy-start(bf16[1,2,384,1536]{3,2,1,0:T(8,128)(2,1)} %param.13) | copy-start | bytes 7077892
  161.9 6.3 %copy-start.8 = (bf16[2048,384]{0,1:T(8,128)(2,1)}, bf16[2048,384]{0,1:T(8,128)(2,1)S(1)}, u32[]{:S(2)}) copy-start(bf16[2048,384]{0,1:T(8,128)(2,1)S(1)} %multiply_convert_fusion.2) | copy-start | bytes 4718596
  161.9 7.4 %copy-start.3 = (bf16[1536,384]{1,0:T(8,128)(2,1)S(1)}, bf16[1536,384]{1,0:T(8,128)(2,1)}, u32[]{:S(2)}) copy-start(bf16[1536,384]{1,0:T(8,128)(2,1)} %get-tuple-element.14) | copy-start | bytes 3538948
  168.2 1.1 copy-start.10
  176.7 1.4 copy-start.9
  178.1 7.4 %copy-start.11 = (bf16[2048,384]{0,1:T(8,128)(2,1)S(1)}, bf16[2048,384]{0,1:T(8,128)(2,1)}, u32[]{:S(2)}) copy-start(bf16[2048,384]{0,1:T(8,128)(2,1)} %copy-done.10) | copy-start | bytes 4718596
  185.5 8.0 %copy-start.2 = (bf16[1,2,1536,384]{3,2,1,0:T(8,128)(2,1)S(1)}, bf16[1,2,1536,384]{3,2,1,0:T(8,128)(2,1)}, u32[]{:S(2)}) copy-start(bf16[1,2,1536,384]{3,2,1,0:T(8,128)(2,1)} %param.12) | copy-start | bytes 7077892
  219.3 48.0 %copy-start.4 = (bf16[1,384,1536]{2,1,0:T(8,128)(2,1)S(1)}, bf16[1,384,1536]{2,1,0:T(8,128)(2,1)}, u32[]{:S(2)}) copy-start(bf16[1,384,1536]{2,1,0:T(8,128)(2,1)} %fusion.9) | copy-start | bytes 3538948
  219.3 48.0 %copy-start.5 = (bf16[1,384,1536]{2,1,0:T(8,128)(2,1)S(1)}, bf16[1,384,1536]{2,1,0:T(8,128)(2,1)}, u32[]{:S(2)}) copy-start(bf16[1,384,1536]{2,1,0:T(8,128)(2,1)} %fusion.8) | copy-start | bytes 3538948
  262.5 10.5 %collective-permute-start = (bf16[1,128,1536]{2,1,0:T(8,128)(2,1)}, bf16[1,128,1536]{2,1,0:T(8,128)(2,1)S(1)}, u32[]{:S(2)}, u32[]{:S(2)}) collective-permute-start(bf16[1,128,1536]{2,1,0:T(8,128)(2,1)} %bitcast.91), channel_id=1, source_target_pairs={{16,0},{0,16},{17,1},{1,17},{18,2},{2,18},{19,3},{3,19},{20,4},{4,... | collective-permute-start | bytes 1179656 | tf_op jit(solution)/shard_map/ppermute | solution.py:17
Sparse Core Ops, SparseCore 0:
  176.8 85.6 reduce-scatter.1
